TPU v7x, 128 devices: a whole 4x4x4 slice. The times are simulated.
128 devices in a mesh: section: 8 (over z, x_lo), dp: 16 (over x_hi, y, core).
Axes of the slice: x: 4 (x_hi: 2, x_lo: 2; x = x_hi * 2 + x_lo), y: 4, z: 4, core: 2. Of those that a mesh axis runs over, the one named last changes fastest.
Arguments:
- acts: bfloat16 [8, 6144, 8192], P('section', 'dp'), may hold values from -6 to 6
- input_grads: bfloat16 [8, 6144, 5120], P('section', 'dp'), may hold values from -6 to 6
- head_grads: bfloat16 [6144, 5120], P('dp'), may hold values from -6 to 6
- weight_grad: bfloat16 [8, 5120, 8192], P('section', None, 'dp'), may hold values from -6 to 6
- sweeps: int32 [8, 52], P('section'), may hold values from 1 to 4
Outputs:
- update: bfloat16 [8, 5120, 8192], P('section', None, 'dp')
Inputs may be any that keep to these rules, and one draw needn't show every extreme that they name: sweeps[s, k] is the number of Newton-Schulz iterations of block k of layer s; every value from 1 to 4 occurs.
All inputs are finite; a program needn't handle non-finite values. Where the computation divides by a largest or mean magnitude, that divisor is 1e-20 or more.
Results may differ from a plain program's by a relative error of at most 0.0067.
Values may be sent and summed in bfloat16 or wider, within the bound.
A program may use at most 128 MiB of HBM per device.

v0:
```python
import jax
import jax.numpy as jnp
from jax import lax
from jax.sharding import PartitionSpec as P

BLOCK = 256
damping = 0.05


def passed_along(block, axis, distance):
    devices = range(lax.axis_size(axis))
    route = [(i - distance, i) for i in devices if i - distance in devices]
    return lax.ppermute(block, axis, route)


def newton_single(matrix, count):
    eye = jnp.eye(matrix.shape[0], dtype=jnp.float32)
    scale = 1.0 / jnp.max(jnp.sum(jnp.abs(matrix), axis=1))

    def sweep(turn, approx):
        inner = 2.0 * eye - jnp.dot(matrix, approx, precision=lax.Precision.HIGHEST)
        return jnp.dot(approx, inner, precision=lax.Precision.HIGHEST)

    return lax.fori_loop(0, count, sweep, scale * eye)


def on_device(acts, input_grads, head_grads, weight_grad, sweeps):
    dp_count = lax.axis_size("dp")
    owner_index = lax.axis_index("dp")
    section_count = lax.axis_size("section")
    section_index = lax.axis_index("section")
    arrived = passed_along(input_grads, "section", -1)
    grads = jnp.where(section_index == section_count - 1, head_grads[None], arrived)[0]
    inputs = acts[0]
    tokens_here = inputs.shape[0]
    hidden_blocks = inputs.shape[1] // BLOCK
    model_blocks = grads.shape[1] // BLOCK
    shaped_a = inputs.reshape(tokens_here, hidden_blocks, BLOCK)
    shaped_g = grads.reshape(tokens_here, model_blocks, BLOCK)
    part_a = jnp.einsum("tkb,tkc->kbc", shaped_a, shaped_a, preferred_element_type=jnp.float32)
    part_g = jnp.einsum("tkb,tkc->kbc", shaped_g, shaped_g, preferred_element_type=jnp.float32)
    partial_value = jnp.concatenate([part_a, part_g], axis=0)
    block_count = partial_value.shape[0]
    capacity = -(-block_count // dp_count)
    slot_total = dp_count * capacity
    counts = sweeps[0]
    block_ids = jnp.arange(block_count, dtype=jnp.int32)
    ordering = jnp.argsort(-counts, stable=True)
    rank_of = jnp.argsort(ordering, stable=True)
    rounds = rank_of // dp_count
    within = rank_of % dp_count
    owner_of = jnp.where(rounds % 2 == 0, within, dp_count - 1 - within)
    slot_of = owner_of * capacity + rounds
    slot_ids = jnp.arange(slot_total, dtype=jnp.int32)
    matches = slot_of[None, :] == slot_ids[:, None]
    block_of = jnp.sum(jnp.where(matches, block_ids[None, :] + 1, 0), axis=1) - 1
    block_of = jnp.where(block_of < 0, block_count, block_of)
    my_blocks = lax.dynamic_slice_in_dim(block_of, owner_index * capacity, capacity)
    zero_block = jnp.zeros((1, BLOCK, BLOCK), jnp.float32)
    outgoing = jnp.take(jnp.concatenate([partial_value, zero_block], axis=0), block_of, axis=0)
    mine = lax.psum_scatter(outgoing, "dp", scatter_dimension=0, tiled=True)
    eye = jnp.eye(BLOCK, dtype=jnp.float32)
    factor = mine / (tokens_here * dp_count) + damping * eye[None]
    padded_counts = jnp.concatenate([counts, jnp.zeros((1,), jnp.int32)])
    my_counts = jnp.take(padded_counts, my_blocks)
    inverted = []
    for position in range(capacity):
        inverted.append(newton_single(factor[position], my_counts[position]))
    inverse = jnp.stack(inverted).astype(jnp.bfloat16)
    every_inverse = lax.all_gather(inverse, "dp", axis=0, tiled=True)
    column_count = weight_grad.shape[2]
    local_blocks = column_count // BLOCK
    column_blocks = owner_index * local_blocks + jnp.arange(local_blocks, dtype=jnp.int32)
    inverse_a = jnp.take(every_inverse, jnp.take(slot_of, column_blocks), axis=0)
    inverse_g = jnp.take(every_inverse, slot_of[hidden_blocks:], axis=0)
    weights = weight_grad[0].reshape(grads.shape[1], local_blocks, BLOCK)
    half = jnp.einsum(
        "dkb,kbc->dkc", weights, inverse_a, preferred_element_type=jnp.float32
    ).astype(jnp.bfloat16)
    half = half.reshape(model_blocks, BLOCK, column_count)
    update = jnp.einsum("kab,kbc->kac", inverse_g, half, preferred_element_type=jnp.float32)
    return update.reshape(grads.shape[1], column_count).astype(jnp.bfloat16)[None]


def solution(mesh):
    return jax.shard_map(
        on_device,
        mesh=mesh,
        in_specs=(
            P("section", "dp", None),
            P("section", "dp", None),
            P("dp", None),
            P("section", None, "dp"),
            P("section", None),
        ),
        out_specs=P("section", None, "dp"),
        check_vma=False,
    )
```

profile of v0, /device:TPU:1, one launch (start us, length us, event | category | flops | bytes accessed | tf_op | source)
XLA Modules:
  0.0 425.9 jit_solution(5902779405749802226)
XLA Ops:
  6.5 6.3 %copy.39 = bf16[1,384,5120]{1,2,0:T(8,128)(2,1)} copy(bf16[1,384,5120]{2,1,0:T(8,128)(2,1)} %param.14) | data formatting | bytes 7864320 | tf_op args[1]
  12.8 1.3 collective-permute-start
  14.1 6.3 %copy.38 = bf16[384,5120]{0,1:T(8,128)(2,1)} copy(bf16[384,5120]{1,0:T(8,128)(2,1)} %param.15) | data formatting | bytes 7864320 | tf_op args[2]
  20.4 7.6 %copy.52 = bf16[48,8,32,256]{3,2,1,0:T(8,128)(2,1)} copy(bf16[48,8,32,256]{3,1,2,0:T(8,128)(2,1)} %bitcast.126) | data formatting | bytes 12582912
  28.0 2.1 sort.31
  30.1 2.1 sort.32
  32.2 0.1 select_reduce_fusion
  32.4 18.6 %fusion.9 = f32[32,256,256]{2,1,0:T(8,128)S(1)} fusion(bf16[384,32,256]{2,1,0:T(8,128)(2,1)} %bitcast.125), kind=kOutput, calls=%fused_computation.25 | convolution fusion | flops 1610612736 | bytes 14680064 | tf_op jit(solution)/shard_map/tkb,tkc->kbc/dot_general | solution.py:40
  51.0 50.3 %collective-permute-done = bf16[1,384,5120]{1,2,0:T(8,128)(2,1)} collective-permute-done((bf16[1,384,5120]{1,2,0:T(8,128)(2,1)}, bf16[1,384,5120]{1,2,0:T(8,128)(2,1)}, u32[]{:S(2)}, u32[]{:S(2)}) %collective-permute-start) | collective-permute-done | bytes 3932192 | tf_op jit(solution)/shard_map/ppermute | solution.py:13
  101.3 3.8 bitcast_select_fusion
  105.1 1.5 fusion.35
  106.6 5.2 %maximum_maximum_fusion = f32[53,256,256]{2,1,0:T(8,128)} fusion(f32[20,256,256]{2,1,0:T(8,128)S(1)} %fusion.35, f32[32,256,256]{2,1,0:T(8,128)S(1)} %fusion.9, f32[53]{0:T(128)S(1)} %pad.8.clone), kind=kLoop, calls=%fused_computation.21 | loop fusion | flops 6946816 | bytes 27525332 | tf_op jit(solution)/shard_map/concatenate | solution.py:60
  111.8 13.7 %gather_fusion = f32[64,256,256]{2,1,0:T(8,128)} fusion(f32[53,256,256]{2,1,0:T(8,128)} %maximum_maximum_fusion, s32[1024]{0:T(1024)S(1)} %pad_clamp_fusion.4), kind=kCustom, calls=%fused_computation | custom fusion | bytes 33554688 | tf_op jit(solution)/shard_map/jit(_take)/gather | solution.py:60
  125.5 11.6 %broadcast_select_fusion = f32[64,256,256]{2,1,0:T(8,128)} fusion(f32[64,256,256]{2,1,0:T(8,128)} %gather_fusion, pred[64]{0:T(512)(128)(4,1)S(1)} %compare_and_fusion.1), kind=kLoop, calls=%fused_computation.22 | loop fusion | flops 4194304 | bytes 33554496 | tf_op jit(solution)/shard_map/jit(_take)/select_n | solution.py:60
  137.2 0.1 copy.41
  137.4 0.1 compare_select_fusion.4
  137.4 0.1 pad_add_fusion
  137.5 0.6 gather_fusion.1
  138.2 0.1 and_select_fusion.2
  138.2 0.7 fusion.34
  138.9 148.8 %reduce-scatter.2.cloned.1.call-done = f32[4,256,256]{2,1,0:T(8,128)} async-done(((f32[64,256,256]{2,1,0:T(8,128)}), f32[4,256,256]{2,1,0:T(8,128)}) %reduce-scatter.2.cloned.1.call-update) | async-done | bytes 1048592 | tf_op jit(solution)/shard_map/reduce_scatter | solution.py:61
  287.7 1.3 multiply_add_fusion
  289.0 0.1 slice_bitcast_fusion.3
  289.1 0.2 abs_reduce_fusion.3
  289.3 0.7 reduce_max.36
  290.8 7.0 %while.44 = (s32[]{:T(128)}, f32[256,256]{0,1:T(8,128)S(1)}, s32[]{:T(128)}, f32[256,256]{1,0:T(8,128)S(1)}, s32[]{:T(128)}) while((s32[]{:T(128)}, f32[256,256]{0,1:T(8,128)S(1)}, s32[]{:T(128)}, f32[256,256]{1,0:T(8,128)S(1)}, s32[]{:T(128)}) %tuple.89), condition=%wide.region_7.8_spmd.clone, body=%wide.region_6.7_spmd.clone.sunk | while | flops 402849792 | bytes 2097213 | solution.py:24
  291.4 0.4 convolution_subtract_fusion.8
  291.8 0.6 convolution_bitcast_fusion.8
  293.0 0.4 convolution_subtract_fusion.8
  293.4 0.6 convolution_bitcast_fusion.8
  294.6 0.4 convolution_subtract_fusion.8
  295.0 0.6 convolution_bitcast_fusion.8
  296.2 0.4 convolution_subtract_fusion.8
  296.6 0.6 convolution_bitcast_fusion.8
  297.8 0.1 copy.42
  297.9 0.7 reduce_max.37
  299.4 5.7 %while.45 = (s32[]{:T(128)}, f32[256,256]{0,1:T(8,128)S(1)}, s32[]{:T(128)}, f32[256,256]{1,0:T(8,128)S(1)}, s32[]{:T(128)}) while((s32[]{:T(128)}, f32[256,256]{0,1:T(8,128)S(1)}, s32[]{:T(128)}, f32[256,256]{1,0:T(8,128)S(1)}, s32[]{:T(128)}) %tuple.86), condition=%wide.region_11.12_spmd.clone, body=%wide.region_10.11_spmd.clone.sunk | while | flops 402849792 | bytes 2097213 | solution.py:24
  300.0 0.4 convolution_subtract_fusion.9
  300.5 0.6 convolution_bitcast_fusion.9
  301.7 0.4 convolution_subtract_fusion.9
  302.2 0.6 convolution_bitcast_fusion.9
  303.4 0.4 convolution_subtract_fusion.9
  303.9 0.6 convolution_bitcast_fusion.9
  305.1 0.1 copy.43
  305.2 0.7 reduce_max.38
  306.6 4.4 %while.46 = (s32[]{:T(128)}, f32[256,256]{0,1:T(8,128)S(1)}, s32[]{:T(128)}, f32[256,256]{1,0:T(8,128)S(1)}, s32[]{:T(128)}) while((s32[]{:T(128)}, f32[256,256]{0,1:T(8,128)S(1)}, s32[]{:T(128)}, f32[256,256]{1,0:T(8,128)S(1)}, s32[]{:T(128)}) %tuple.83), condition=%wide.region_15.16_spmd.clone, body=%wide.region_14.15_spmd.clone.sunk | while | flops 402849792 | bytes 2097213 | solution.py:24
  307.4 0.4 convolution_subtract_fusion.10
  307.8 0.6 convolution_bitcast_fusion.10
  309.1 0.4 convolution_subtract_fusion.10
  309.5 0.6 convolution_bitcast_fusion.10
  311.1 0.1 copy.44
  311.2 0.7 reduce_max.39
  312.6 0.6 while.47
  313.2 0.1 copy.45
  313.3 0.9 pad_maximum_fusion
  314.3 0.6 gather_fusion.3
  314.9 8.3 %reshape_squeeze.11 = bf16[5120,2,256]{2,1,0:T(2,128)(2,1)} reshape(bf16[1,5120,512]{2,1,0:T(8,128)(2,1)} %param.16) | data formatting | bytes 10485760 | tf_op jit(solution)/shard_map/reshape;squeeze | solution.py:76
  323.2 0.1 compare_and_fusion.2
  323.3 64.0 %all-gather.2.cloned.1.call-done = bf16[64,256,256]{2,1,0:T(8,128)(2,1)} async-done(((bf16[4,256,256]{2,1,0:T(8,128)(2,1)}), bf16[64,256,256]{2,1,0:T(8,128)(2,1)}) %all-gather.2.cloned.1.call-update) | async-done | bytes 8388624 | tf_op jit(solution)/shard_map/all_gather | solution.py:70
  387.3 3.9 gather_fusion.4
  391.2 6.5 %fusion.8 = bf16[5120,2,256]{0,2,1:T(8,128)(2,1)} fusion(bf16[5120,2,256]{2,1,0:T(2,128)(2,1)} %reshape_squeeze.11, bf16[2,256,256]{2,1,0:T(8,128)(2,1)S(1)} %gather_fusion.4, pred[2]{0:T(512)(128)(4,1)S(1)} %compare_and_fusion), kind=kOutput, calls=%fused_computation.24 | convolution fusion | flops 1344929792 | bytes 10747906 | tf_op jit(solution)/shard_map/dkb,kbc->dkc/dot_general | solution.py:77
  397.7 10.0 %reshape.165 = bf16[20,256,512]{1,0,2:T(8,128)(2,1)} reshape(bf16[5120,2,256]{0,2,1:T(8,128)(2,1)} %fusion.8) | data formatting | bytes 10485760 | tf_op jit(solution)/shard_map/reshape | solution.py:80
  407.7 4.1 gather_fusion.2
  411.8 7.2 %fusion.14 = bf16[20,256,512]{2,1,0:T(8,128)(2,1)} fusion(bf16[20,256,512]{1,0,2:T(8,128)(2,1)} %reshape.165, bf16[20,256,256]{2,1,0:T(8,128)(2,1)S(1)} %gather_fusion.2, pred[20]{0:T(512)(128)(4,1)S(1)} %get-tuple-element.205), kind=kOutput, calls=%fused_computation.31 | convolution fusion | flops 1346109440 | bytes 13107220 | tf_op jit(solution)/shard_map/kab,kbc->kac/dot_general | solution.py:81
  (36 shorter events, 0.5 us)
Async XLA Ops:
  6.5 281.1 %reduce-scatter.2.cloned.1.call-start = ((), (), s32[]{:S(2)}) async-start(), calls=%async_computation.1 | async-start | bytes 17825792 | tf_op jit(solution)/shard_map/reduce_scatter | solution.py:61
  12.8 88.5 %collective-permute-start = (bf16[1,384,5120]{1,2,0:T(8,128)(2,1)}, bf16[1,384,5120]{1,2,0:T(8,128)(2,1)}, u32[]{:S(2)}, u32[]{:S(2)}) collective-permute-start(bf16[1,384,5120]{1,2,0:T(8,128)(2,1)} %copy.39), channel_id=1, source_target_pairs={{16,0},{32,16},{48,32},{64,48},{80,64},{96,80},{112,96},{17,1},{33... | collective-permute-start | bytes 11796488 | tf_op jit(solution)/shard_map/ppermute | solution.py:13
  20.4 7.6 %copy-start = (s32[1,52]{1,0:T(1,128)S(1)}, s32[1,52]{1,0:T(1,128)}, u32[]{:S(2)}) copy-start(s32[1,52]{1,0:T(1,128)} %param.17) | copy-start | bytes 628
  137.1 250.2 %all-gather.2.cloned.1.call-start = ((), (), s32[]{:S(2)}) async-start(), calls=%async_computation.2 | async-start | bytes 8912896 | tf_op jit(solution)/shard_map/all_gather | solution.py:70
Sparse Core Ops, SparseCore 0:
  137.2 150.3 reduce-scatter.1
  314.4 72.8 all-gather.1
where the time goes:
time: 427 us; the launch traced here: 426 us
  waiting for transfers between devices  263 us (62%)
  local copies, waits for them, and re-layouts  62.9 us (15%)
  matrix products  43 us (10%)
  other arithmetic  30.5 us (7%)
  between operations  16.6 us (4%)
  loops' own time  8.52 us (2%)
    reduce_scatter x1, waiting for transfers between devices, on_device(): mine = lax.psum_scatter(outgoing, 'dp', scatter_dimension=0, tiled=True)  149 us
    all_gather x1, waiting for transfers between devices, on_device(): every_inverse = lax.all_gather(inverse, 'dp', axis=0, tiled=True)  64 us
    ppermute x1, waiting for transfers between devices, passed_along(): return lax.ppermute(block, axis, route)  50.3 us
    unnamed x5, local copies, waits for them, and re-layouts  20.1 us
    dot_general x1, matrix products, on_device(): jnp.einsum('tkb,tkc->kbc', shaped_a, shaped_a, preferred_element_type=jnp...  18.6 us
    gather x1, local copies, waits for them, and re-layouts, on_device(): jnp.take(jnp.concatenate([partial_value, zero_block], axis=0), block_of,...  13.7 us
    select_n x2, other arithmetic, on_device(): jnp.take(jnp.concatenate([partial_value, zero_block], axis=0), block_of,...  11.6 us
    reshape x1, local copies, waits for them, and re-layouts, on_device(): half = half.reshape(model_blocks, BLOCK, column_count)  9.95 us
  transfers between devices with their start and end apart: 3, of which 3 were waited for; matrix products, arithmetic and copies ran while one was open for 11% of the time, Pallas kernels for 0%

commit v1 on v0

--- a/solution.py
+++ b/solution.py
@@ -67,7 +67,9 @@
     for position in range(capacity):
         inverted.append(newton_single(factor[position], my_counts[position]))
     inverse = jnp.stack(inverted).astype(jnp.bfloat16)
-    every_inverse = lax.all_gather(inverse, "dp", axis=0, tiled=True)
+    every_inverse = jnp.concatenate(
+        lax.all_to_all(jnp.stack([inverse] * lax.axis_size("dp")), "dp", 0, 0), axis=0
+    )
     column_count = weight_grad.shape[2]
     local_blocks = column_count // BLOCK
     column_blocks = owner_index * local_blocks + jnp.arange(local_blocks, dtype=jnp.int32)

time: 427 us -> 491 us (1.15); the launches traced: 426 us -> 483 us
  waiting for transfers between devices: 263 us -> 313 us
    all_to_all x0 -> x1, waiting for transfers between devices: none -> 114 us  [on_device(): lax.all_to_all(jnp.stack([inverse] * lax.axis_size('dp')), 'dp', 0, 0)]
    all_gather x1 -> x0, waiting for transfers between devices: 64 us -> none  [on_device(): every_inverse = lax.all_gather(inverse, 'dp', axis=0, tiled=True)]
  transfers between devices with their start and end apart: 3 -> 3, of which waited for: 3 -> 3; matrix products, arithmetic and copies ran while one was open for 11% -> 10% of each run, Pallas kernels for 0% -> 0%
where the time goes in v1:
time: 491 us; the launch traced here: 483 us
  waiting for transfers between devices  313 us (64%)
  local copies, waits for them, and re-layouts  67 us (14%)
  matrix products  43 us (9%)
  other arithmetic  29.7 us (6%)
  between operations  16.6 us (3%)
  loops' own time  8.52 us (2%)
  starting transfers between devices  5.94 us (1%)
    reduce_scatter x1, waiting for transfers between devices, on_device(): mine = lax.psum_scatter(outgoing, 'dp', scatter_dimension=0, tiled=True)  149 us
    all_to_all x1, waiting for transfers between devices, on_device(): lax.all_to_all(jnp.stack([inverse] * lax.axis_size('dp')), 'dp', 0, 0)  114 us
    ppermute x1, waiting for transfers between devices, passed_along(): return lax.ppermute(block, axis, route)  50.3 us
    unnamed x5, local copies, waits for them, and re-layouts  20.1 us
    dot_general x1, matrix products, on_device(): jnp.einsum('tkb,tkc->kbc', shaped_a, shaped_a, preferred_element_type=jnp...  18.6 us
    gather x1, local copies, waits for them, and re-layouts, on_device(): jnp.take(jnp.concatenate([partial_value, zero_block], axis=0), block_of,...  13.7 us
    select_n x2, other arithmetic, on_device(): jnp.take(jnp.concatenate([partial_value, zero_block], axis=0), block_of,...  11.6 us
    reshape x1, local copies, waits for them, and re-layouts, on_device(): half = half.reshape(model_blocks, BLOCK, column_count)  9.95 us
  transfers between devices with their start and end apart: 3, of which 3 were waited for; matrix products, arithmetic and copies ran while one was open for 10% of the time, Pallas kernels for 0%

profile of v1, /device:TPU:1, one launch (start us, length us, event | category | flops | bytes accessed | tf_op | source)
XLA Modules:
  0.0 483.4 jit_solution(2079807146512385781)
XLA Ops:
  6.5 6.3 %copy.27 = bf16[1,384,5120]{1,2,0:T(8,128)(2,1)} copy(bf16[1,384,5120]{2,1,0:T(8,128)(2,1)} %param.14) | data formatting | bytes 7864320 | tf_op args[1]
  12.8 1.3 collective-permute-start
  14.1 6.3 %copy.26 = bf16[384,5120]{0,1:T(8,128)(2,1)} copy(bf16[384,5120]{1,0:T(8,128)(2,1)} %param.15) | data formatting | bytes 7864320 | tf_op args[2]
  20.4 7.6 %copy.37 = bf16[48,8,32,256]{3,2,1,0:T(8,128)(2,1)} copy(bf16[48,8,32,256]{3,1,2,0:T(8,128)(2,1)} %bitcast.123) | data formatting | bytes 12582912
  28.0 2.1 sort.31
  30.1 2.1 sort.32
  32.1 0.1 pad.8.clone
  32.2 0.1 select_reduce_fusion
  32.4 18.6 %fusion.9 = f32[32,256,256]{2,1,0:T(8,128)S(1)} fusion(bf16[384,32,256]{2,1,0:T(8,128)(2,1)} %bitcast.122), kind=kOutput, calls=%fused_computation.25 | convolution fusion | flops 1610612736 | bytes 14680064 | tf_op jit(solution)/shard_map/tkb,tkc->kbc/dot_general | solution.py:40
  51.0 50.3 %collective-permute-done = bf16[1,384,5120]{1,2,0:T(8,128)(2,1)} collective-permute-done((bf16[1,384,5120]{1,2,0:T(8,128)(2,1)}, bf16[1,384,5120]{1,2,0:T(8,128)(2,1)}, u32[]{:S(2)}, u32[]{:S(2)}) %collective-permute-start) | collective-permute-done | bytes 3932192 | tf_op jit(solution)/shard_map/ppermute | solution.py:13
  101.3 3.8 bitcast_select_fusion
  105.1 1.5 fusion.35
  106.6 5.2 %maximum_maximum_fusion = f32[53,256,256]{2,1,0:T(8,128)} fusion(f32[20,256,256]{2,1,0:T(8,128)S(1)} %fusion.35, f32[32,256,256]{2,1,0:T(8,128)S(1)} %fusion.9, f32[53]{0:T(128)S(1)} %pad.8.clone), kind=kLoop, calls=%fused_computation.21 | loop fusion | flops 6946816 | bytes 27525332 | tf_op jit(solution)/shard_map/concatenate | solution.py:60
  111.8 13.7 %gather_fusion = f32[64,256,256]{2,1,0:T(8,128)} fusion(f32[53,256,256]{2,1,0:T(8,128)} %maximum_maximum_fusion, s32[1024]{0:T(1024)S(1)} %pad_clamp_fusion.4), kind=kCustom, calls=%fused_computation | custom fusion | bytes 33554688 | tf_op jit(solution)/shard_map/jit(_take)/gather | solution.py:60
  125.5 11.6 %broadcast_select_fusion = f32[64,256,256]{2,1,0:T(8,128)} fusion(f32[64,256,256]{2,1,0:T(8,128)} %gather_fusion, pred[64]{0:T(512)(128)(4,1)S(1)} %compare_and_fusion.1), kind=kLoop, calls=%fused_computation.22 | loop fusion | flops 4194304 | bytes 33554496 | tf_op jit(solution)/shard_map/jit(_take)/select_n | solution.py:60
  137.2 0.1 copy.29
  137.3 0.1 compare_select_fusion.4
  137.4 0.1 pad_add_fusion
  137.5 0.6 gather_fusion.1
  138.1 0.1 and_select_fusion.2
  138.2 0.7 fusion.34
  138.9 148.8 %reduce-scatter.2.cloned.1.call-done = f32[4,256,256]{2,1,0:T(8,128)} async-done(((f32[64,256,256]{2,1,0:T(8,128)}), f32[4,256,256]{2,1,0:T(8,128)}) %reduce-scatter.2.cloned.1.call-update) | async-done | bytes 1048592 | tf_op jit(solution)/shard_map/reduce_scatter | solution.py:61
  287.7 1.3 multiply_add_fusion
  289.0 0.1 slice_bitcast_fusion.3
  289.1 0.2 abs_reduce_fusion.3
  289.3 0.7 reduce_max.36
  290.8 7.0 %while.44 = (s32[]{:T(128)}, f32[256,256]{0,1:T(8,128)S(1)}, s32[]{:T(128)}, f32[256,256]{1,0:T(8,128)S(1)}, s32[]{:T(128)}) while((s32[]{:T(128)}, f32[256,256]{0,1:T(8,128)S(1)}, s32[]{:T(128)}, f32[256,256]{1,0:T(8,128)S(1)}, s32[]{:T(128)}) %tuple.89), condition=%wide.region_7.8_spmd.clone, body=%wide.region_6.7_spmd.clone.sunk | while | flops 402849792 | bytes 2097213 | solution.py:24
  291.4 0.4 convolution_subtract_fusion.8
  291.8 0.6 convolution_bitcast_fusion.8
  293.0 0.4 convolution_subtract_fusion.8
  293.4 0.6 convolution_bitcast_fusion.8
  294.6 0.4 convolution_subtract_fusion.8
  295.0 0.6 convolution_bitcast_fusion.8
  296.2 0.4 convolution_subtract_fusion.8
  296.6 0.6 convolution_bitcast_fusion.8
  297.8 0.7 reduce_max.37
  299.3 5.7 %while.45 = (s32[]{:T(128)}, f32[256,256]{0,1:T(8,128)S(1)}, s32[]{:T(128)}, f32[256,256]{1,0:T(8,128)S(1)}, s32[]{:T(128)}) while((s32[]{:T(128)}, f32[256,256]{0,1:T(8,128)S(1)}, s32[]{:T(128)}, f32[256,256]{1,0:T(8,128)S(1)}, s32[]{:T(128)}) %tuple.86), condition=%wide.region_11.12_spmd.clone, body=%wide.region_10.11_spmd.clone.sunk | while | flops 402849792 | bytes 2097213 | solution.py:24
  300.0 0.4 convolution_subtract_fusion.9
  300.4 0.6 convolution_bitcast_fusion.9
  301.7 0.4 convolution_subtract_fusion.9
  302.1 0.6 convolution_bitcast_fusion.9
  303.4 0.4 convolution_subtract_fusion.9
  303.8 0.6 convolution_bitcast_fusion.9
  305.0 0.7 reduce_max.38
  306.5 4.4 while.46
  307.2 0.4 convolution_subtract_fusion.10
  307.6 0.6 convolution_bitcast_fusion.10
  309.0 0.4 convolution_subtract_fusion.10
  309.4 0.6 convolution_bitcast_fusion.10
  310.9 0.7 reduce_max.39
  312.4 0.6 while.47
  313.0 0.1 pad_maximum_fusion
  313.0 0.2 copy.30
  313.3 4.2 stack.17
  317.5 4.7 all-to-all-start
  322.2 0.6 gather_fusion.3
  322.8 8.3 %reshape_squeeze.11 = bf16[5120,2,256]{2,1,0:T(2,128)(2,1)} reshape(bf16[1,5120,512]{2,1,0:T(8,128)(2,1)} %param.16) | data formatting | bytes 10485760 | tf_op jit(solution)/shard_map/reshape;squeeze | solution.py:78
  331.1 0.1 compare_and_fusion.2
  331.2 113.6 %all-to-all-done = bf16[16,4,256,256]{3,2,1,0:T(8,128)(2,1)} async-done(((bf16[16,4,256,256]{3,2,1,0:T(8,128)(2,1)}), bf16[16,4,256,256]{3,2,1,0:T(8,128)(2,1)}, u32[]{:S(2)}, u32[]{:S(2)}) %all-to-all-start) | async-done | bytes 8388640 | tf_op jit(solution)/shard_map/all_to_all | solution.py:71
  444.8 3.9 gather_fusion.4
  448.8 6.5 %fusion.8 = bf16[5120,2,256]{0,2,1:T(8,128)(2,1)} fusion(bf16[5120,2,256]{2,1,0:T(2,128)(2,1)} %reshape_squeeze.11, bf16[2,256,256]{2,1,0:T(8,128)(2,1)S(1)} %gather_fusion.4, pred[2]{0:T(512)(128)(4,1)S(1)} %compare_and_fusion), kind=kOutput, calls=%fused_computation.24 | convolution fusion | flops 1344929792 | bytes 10747906 | tf_op jit(solution)/shard_map/dkb,kbc->dkc/dot_general | solution.py:79
  455.3 10.0 %reshape.190 = bf16[20,256,512]{1,0,2:T(8,128)(2,1)} reshape(bf16[5120,2,256]{0,2,1:T(8,128)(2,1)} %fusion.8) | data formatting | bytes 10485760 | tf_op jit(solution)/shard_map/reshape | solution.py:82
  465.2 4.1 gather_fusion.2
  469.3 7.2 %fusion.14 = bf16[20,256,512]{2,1,0:T(8,128)(2,1)} fusion(bf16[20,256,512]{1,0,2:T(8,128)(2,1)} %reshape.190, bf16[20,256,256]{2,1,0:T(8,128)(2,1)S(1)} %gather_fusion.2, pred[20]{0:T(512)(128)(4,1)S(1)} %get-tuple-element.205), kind=kOutput, calls=%fused_computation.31 | convolution fusion | flops 1346109440 | bytes 13107220 | tf_op jit(solution)/shard_map/kab,kbc->kac/dot_general | solution.py:83
  (37 shorter events, 0.5 us)
Async XLA Ops:
  6.5 281.1 %reduce-scatter.2.cloned.1.call-start = ((), (), s32[]{:S(2)}) async-start(), calls=%async_computation.2 | async-start | bytes 17825792 | tf_op jit(solution)/shard_map/reduce_scatter | solution.py:61
  12.8 88.5 %collective-permute-start = (bf16[1,384,5120]{1,2,0:T(8,128)(2,1)}, bf16[1,384,5120]{1,2,0:T(8,128)(2,1)}, u32[]{:S(2)}, u32[]{:S(2)}) collective-permute-start(bf16[1,384,5120]{1,2,0:T(8,128)(2,1)} %copy.27), channel_id=1, source_target_pairs={{16,0},{32,16},{48,32},{64,48},{80,64},{96,80},{112,96},{17,1},{33... | collective-permute-start | bytes 11796488 | tf_op jit(solution)/shard_map/ppermute | solution.py:13
  20.4 7.6 %copy-start = (s32[1,52]{1,0:T(1,128)S(1)}, s32[1,52]{1,0:T(1,128)}, u32[]{:S(2)}) copy-start(s32[1,52]{1,0:T(1,128)} %param.17) | copy-start | bytes 628
  317.5 127.3 %all-to-all-start = ((bf16[16,4,256,256]{3,2,1,0:T(8,128)(2,1)}), bf16[16,4,256,256]{3,2,1,0:T(8,128)(2,1)}, u32[]{:S(2)}, u32[]{:S(2)}) async-start(bf16[16,4,256,256]{3,2,1,0:T(8,128)(2,1)} %stack.17), calls=%async_computation.1 | async-start | bytes 16777216 | tf_op jit(solution)/shard_map/all_to_all | solution.py:71
Sparse Core Ops, SparseCore 0:
  137.2 150.3 reduce-scatter.1
